TPU v7x, 32 devices: a 4x4x1 block of a 4x4x8 slice. The times are simulated.
32 devices in a mesh: dp: 1 (over z), ep: 32 (over y, x, core).
Axes of the slice: x: 4, y: 4, z: 1, core: 2. Of those that a mesh axis runs over, the one named last changes fastest.
The devices are a block of a 4x4x8 slice.
Arguments:
- tok_x: bfloat16 [32768, 1024], P(('dp', 'ep'))
- expert_ids: int32 [32768, 8], P(('dp', 'ep'))
- gates: float32 [32768, 8], P(('dp', 'ep'))
- hot_tok: int32 [32768], P(('dp', 'ep'))
- hot_gates: float32 [32768], P(('dp', 'ep'))
- w_gate: bfloat16 [32, 1024, 512], P('ep')
- w_up: bfloat16 [32, 1024, 512], P('ep')
- w_down: bfloat16 [32, 512, 1024], P('ep')
Outputs:
- output: bfloat16 [32768, 1024], P(('dp', 'ep'))
All inputs are finite; a program needn't handle non-finite values.
Results may differ from a plain program's by a relative error of at most 0.00796467.
Values are sent between devices in bfloat16 or wider.
A program may use at most 768 MiB of HBM per device.

v0:
```python
import jax
import jax.numpy as jnp
from jax import lax
from jax.sharding import PartitionSpec as P


def route_plan(flat_ids, num_experts, cold_cap):
    routes = flat_ids.shape[0]
    sort_order = jnp.argsort(flat_ids, stable=True)
    exp_counts = jnp.bincount(flat_ids, length=num_experts).astype(jnp.int32)
    exp_starts = jnp.cumsum(exp_counts) - exp_counts
    slot_pos = jnp.arange(cold_cap, dtype=jnp.int32)
    filled = slot_pos[None, :] < exp_counts[:, None]
    sorted_pos = jnp.minimum(exp_starts[:, None] + slot_pos[None, :], routes - 1)
    src_route = sort_order[sorted_pos]
    route_rank = jnp.zeros((routes,), jnp.int32).at[sort_order].set(jnp.arange(routes, dtype=jnp.int32))
    route_slot = flat_ids * cold_cap + route_rank - exp_starts[flat_ids]
    return src_route, filled, route_slot


def swiglu_rows(in_rows, w_gate_e, w_up_e, w_down_e):
    gate_act = jnp.einsum('...d,df->...f', in_rows, w_gate_e, preferred_element_type=jnp.float32)
    up_act = jnp.einsum('...d,df->...f', in_rows, w_up_e, preferred_element_type=jnp.float32)
    hidden = (jax.nn.silu(gate_act) * up_act).astype(jnp.bfloat16)
    return jnp.einsum('...f,fd->...d', hidden, w_down_e, preferred_element_type=jnp.float32).astype(jnp.bfloat16)


def combine_rows(out_rows, route_slot, gates_loc, hot_loc, hot_g_loc):
    num_tokens, top_k = gates_loc.shape
    hot_count = hot_loc.shape[0]
    cold_total = out_rows.shape[0] - hot_count
    hot_index = jnp.zeros((num_tokens,), jnp.int32).at[hot_loc].set(jnp.arange(hot_count, dtype=jnp.int32))
    hot_weight = jnp.zeros((num_tokens,), jnp.float32).at[hot_loc].set(hot_g_loc)
    all_slots = jnp.concatenate([route_slot.reshape(num_tokens, top_k), (cold_total + hot_index)[:, None]], axis=1)
    all_gates = jnp.concatenate([gates_loc, hot_weight[:, None]], axis=1)
    picked = out_rows[all_slots]
    return jnp.einsum('tk,tkd->td', all_gates, picked, preferred_element_type=jnp.float32).astype(jnp.bfloat16)


def solution(mesh):
    group_size = mesh.shape['ep']
    row_spec = P(('dp', 'ep'), None)
    list_spec = P(('dp', 'ep'))
    expert_spec = P('ep', None, None)

    def local_layer(x_loc, ids_loc, gates_loc, hot_loc, hot_g_loc, wg_loc, wu_loc, wd_loc):
        local_experts = wg_loc.shape[0]
        d_model = x_loc.shape[1]
        num_experts = local_experts * group_size
        num_tokens, top_k = ids_loc.shape
        cold_cap = (num_tokens * top_k + num_experts - 2) // (num_experts - 1)
        block_rows = local_experts * cold_cap
        src_route, filled, route_slot = route_plan(ids_loc.reshape(num_tokens * top_k), num_experts, cold_cap)
        cold_buf = jnp.where(filled[:, :, None], x_loc[src_route // top_k], 0)
        hot_buf = x_loc[hot_loc]
        to_owner = jnp.where(jnp.arange(group_size)[:, None, None] == 0, hot_buf[None], 0)
        send_buf = jnp.concatenate([cold_buf.reshape(group_size, block_rows, d_model), to_owner], axis=1)
        recv_buf = lax.all_to_all(send_buf, 'ep', 0, 0, tiled=True)
        cold_in = recv_buf[:, :block_rows].reshape(group_size, local_experts, cold_cap, d_model)
        gate_act = jnp.einsum('slcd,ldf->slcf', cold_in, wg_loc, preferred_element_type=jnp.float32)
        up_act = jnp.einsum('slcd,ldf->slcf', cold_in, wu_loc, preferred_element_type=jnp.float32)
        hidden = (jax.nn.silu(gate_act) * up_act).astype(jnp.bfloat16)
        cold_out = jnp.einsum('slcf,lfd->slcd', hidden, wd_loc, preferred_element_type=jnp.float32).astype(jnp.bfloat16)
        hot_out = lax.cond(lax.axis_index('ep') == 0,
                           lambda hot_in: swiglu_rows(hot_in, wg_loc[0], wu_loc[0], wd_loc[0]),
                           jnp.zeros_like, recv_buf[:, block_rows:])
        back_buf = jnp.concatenate([cold_out.reshape(group_size, block_rows, d_model), hot_out], axis=1)
        ret_buf = lax.all_to_all(back_buf, 'ep', 0, 0, tiled=True)
        out_rows = jnp.concatenate([ret_buf[:, :block_rows].reshape(num_experts * cold_cap, d_model),
                                    ret_buf[0, block_rows:]], axis=0)
        return combine_rows(out_rows, route_slot, gates_loc, hot_loc, hot_g_loc)

    return jax.shard_map(local_layer, mesh=mesh,
                         in_specs=(row_spec, row_spec, row_spec, list_spec, list_spec, expert_spec, expert_spec, expert_spec),
                         out_specs=row_spec, check_vma=False)
```

profile of v0, /device:TPU:106, one launch (start us, length us, event | category | flops | bytes accessed | tf_op | source)
XLA Modules:
  0.0 2865.4 jit_solution(1683446728493321757)
XLA Ops:
  0.0 0.0 copy-start
  0.0 1.1 copy.14
  1.1 0.3 reshape.309
  1.4 0.3 reshape.308
  1.7 0.0 copy-start.7
  1.7 1.3 broadcast_clamp_fusion.1
  3.0 57.0 %scatter_custom_fusion.1 = s32[32]{0:T(128)S(1)} fusion(s32[8192]{0:T(1024)S(1)} %bitcast.117, s32[8192]{0:T(1024)S(1)} %broadcast.256, s32[]{:T(128)} %constant.21.clone.1), kind=kCustom, calls=%fused_computation.102 | custom fusion | flops 8192 | bytes 132 | tf_op jit(solution)/shard_map/scatter-add | solution.py:10
  60.0 0.1 iota_compare_fusion
  60.1 0.1 copy.16
  60.2 0.1 reduce-window.9
  60.2 0.1 reduce
  60.4 0.6 copy-done.5
  60.9 0.1 compare_select_fusion.3
  61.0 0.1 reshape.319
  61.2 6.8 sort.17
  68.0 44.1 %gather_fusion = s32[8480]{0:T(1024)S(1)} fusion(s32[8192]{0:T(1024)S(1)} %get-tuple-element.21, s32[9216]{0:T(1024)S(1)} %pad_clamp_fusion.1), kind=kCustom, calls=%fused_computation | custom fusion | bytes 101760 | tf_op jit(solution)/shard_map/gather | solution.py:15
  112.1 0.1 gather.18
  112.3 0.1 reshape.327
  112.4 0.0 copy-done
  112.4 5.3 gather_fusion.2
  117.8 0.0 copy-done.9
  117.8 27.0 gather_fusion.1
  144.8 22.5 reshape.326
  167.3 20.9 broadcast_select_fusion
  188.2 14.7 broadcast_select_fusion.1
  202.9 56.5 %pad_maximum_fusion = bf16[32,1289,1024]{2,1,0:T(8,128)(2,1)} fusion(bf16[32,1024,1024]{2,1,0:T(8,128)(2,1)} %broadcast_select_fusion, bf16[32,265,1024]{2,1,0:T(8,128)(2,1)} %broadcast_select_fusion.1), kind=kLoop, calls=%fused_computation.19 | loop fusion | flops 168951808 | bytes 168951808 | tf_op jit(solution)/shard_map/concatenate | solution.py:57
  259.4 0.0 copy-start.12
  259.4 0.0 copy-start.13
  259.5 0.0 copy-start.14
  259.5 7.5 all-to-all-start
  267.0 1081.3 %all-to-all-done = bf16[32,1289,1024]{2,1,0:T(8,128)(2,1)} async-done(((bf16[32,1289,1024]{2,1,0:T(8,128)(2,1)}), bf16[32,1289,1024]{2,1,0:T(8,128)(2,1)}, u32[]{:S(2)}, u32[]{:S(2)}) %all-to-all-start) | async-done | bytes 84475936 | tf_op jit(solution)/shard_map/all_to_all | solution.py:58
  1348.2 0.0 copy-done.13
  1348.3 29.5 %conditional.1 = (bf16[32,1024,1024]{2,1,0:T(8,128)(2,1)}) conditional(s32[]{:T(128)} %convert_element_type.27, () %tuple.11, (bf16[1,1024,512]{2,1,0:T(8,128)(2,1)S(1)}, bf16[32,1289,1024]{2,1,0:T(8,128)(2,1)}, bf16[1,1024,512]{2,1,0:T(8,128)(2,1)S(1)}, bf16[1,512,1024]{2,1,0:T(8,128)(2,1)S(1)}) %tuple.73), branch_computations={%region_4.5_spmd, %region_5.6_spmd} | conditional | flops 103213432832 | bytes 338690048 | solution.py:64
  1348.3 21.1 broadcast.180
  1377.7 16.7 fusion.18
  1394.4 27.1 convolution_convert_fusion.1
  1421.5 57.1 %pad_maximum_fusion.1 = bf16[32,1289,1024]{2,1,0:T(8,128)(2,1)} fusion(bf16[32,1024,1024]{2,1,0:T(8,128)(2,1)} %get-tuple-element.84, bf16[32,265,1024]{2,1,0:T(8,128)(2,1)} %convolution_convert_fusion.1), kind=kLoop, calls=%fused_computation.20 | loop fusion | flops 168951808 | bytes 168951808 | tf_op jit(solution)/shard_map/concatenate | solution.py:67
  1478.6 0.0 copy-start.11
  1478.6 125.4 %all-to-all-start.1 = ((bf16[32,1289,1024]{2,1,0:T(8,128)(2,1)}), bf16[32,1289,1024]{2,1,0:T(8,128)(2,1)}, u32[]{:S(2)}, u32[]{:S(2)}) async-start(bf16[32,1289,1024]{2,1,0:T(8,128)(2,1)} %pad_maximum_fusion.1), calls=%async_computation.1 | async-start | bytes 169869312 | tf_op jit(solution)/shard_map/all_to_all | solution.py:68
  1604.1 16.4 scatter_custom_fusion
  1620.5 0.4 copy.19
  1621.0 4.4 scatter_custom_fusion.3
  1625.4 0.0 copy-done.3
  1625.5 30.5 %scatter_custom_fusion.2 = s32[8192]{0:T(1024)S(1)} fusion(s32[8192]{0:T(1024)S(1)} %compare_select_fusion.10, s32[8192]{0:T(1024)S(1)} %iota.27, s32[]{:T(128)} %constant.21.clone.1), kind=kCustom, calls=%fused_computation.91 | custom fusion | bytes 32772 | tf_op jit(solution)/shard_map/scatter | solution.py:16
  1655.9 0.7 fusion.44
  1656.7 0.7 fusion.43
  1657.4 4.6 compare_select_fusion.4
  1662.0 2.5 compare_reduce_fusion.24
  1664.5 15.9 select_subtract_fusion
  1680.4 0.3 concatenate.42
  1680.7 0.2 copy.17
  1680.9 0.1 compare_select_fusion
  1680.9 0.2 copy.18
  1681.2 0.4 reshape.382
  1681.5 1017.4 %all-to-all-done.1 = bf16[32,1289,1024]{2,1,0:T(8,128)(2,1)} async-done(((bf16[32,1289,1024]{2,1,0:T(8,128)(2,1)}), bf16[32,1289,1024]{2,1,0:T(8,128)(2,1)}, u32[]{:S(2)}, u32[]{:S(2)}) %all-to-all-start.1) | async-done | bytes 84475936 | tf_op jit(solution)/shard_map/all_to_all | solution.py:68
  2698.9 14.5 slice.59
  2713.4 22.3 reshape.316
  2735.7 2.2 slice_bitcast_fusion
  2737.9 23.8 pad_maximum_fusion.2
  2761.7 54.6 %gather_fusion.3 = bf16[9216,1024]{1,0:T(8,128)(2,1)} fusion(bf16[9504,1024]{1,0:T(8,128)(2,1)} %pad_maximum_fusion.2, s32[9216]{0:T(1024)S(1)} %broadcast_clamp_fusion), kind=kCustom, calls=%fused_computation.3 | custom fusion | bytes 37785600 | tf_op jit(solution)/shard_map/gather | solution.py:36
  2816.3 34.1 %reshape.381 = bf16[1024,9,1024]{2,1,0:T(8,128)(2,1)} reshape(bf16[9216,1024]{1,0:T(8,128)(2,1)} %gather_fusion.3) | data formatting | bytes 37748736 | tf_op jit(solution)/shard_map/gather | solution.py:36
  2850.4 12.7 fusion.45
  2863.1 2.1 copy.22
  2865.2 0.0 copy-done.1
  (32 shorter events, 0.2 us)
Async XLA Ops:
  0.0 112.4 %copy-start = (bf16[1024,1024]{1,0:T(8,128)(2,1)S(1)}, bf16[1024,1024]{1,0:T(8,128)(2,1)}, u32[]{:S(2)}) copy-start(bf16[1024,1024]{1,0:T(8,128)(2,1)} %param.10) | copy-start | bytes 6291460
  1.4 116.4 %copy-start.9 = (s32[8192]{0:T(1024)}, s32[8192]{0:T(1024)S(1)}, u32[]{:S(2)}) copy-start(s32[8192]{0:T(1024)S(1)} %reshape.309) | copy-start | bytes 98308
  1.7 116.1 %copy-start.7 = (s32[8192,1]{0,1:T(1,128)}, s32[8192,1]{0,1:T(1,128)S(1)}, u32[]{:S(2)}) copy-start(s32[8192,1]{0,1:T(1,128)S(1)} %reshape.308) | copy-start | bytes 98308
  60.4 0.6 copy-start.5
  68.0 49.8 %copy-start.2 = (s32[8192]{0:T(1024)}, s32[8192]{0:T(1024)S(1)}, u32[]{:S(2)}) copy-start(s32[8192]{0:T(1024)S(1)} %get-tuple-element.21) | copy-start | bytes 98308
  144.8 22.5 copy-start.4
  259.4 1088.8 %copy-start.12 = (bf16[1,1024,512]{2,1,0:T(8,128)(2,1)S(1)}, bf16[1,1024,512]{2,1,0:T(8,128)(2,1)}, u32[]{:S(2)}) copy-start(bf16[1,1024,512]{2,1,0:T(8,128)(2,1)} %param.16) | copy-start | bytes 3145732
  259.4 1088.8 %copy-start.13 = (bf16[1,1024,512]{2,1,0:T(8,128)(2,1)S(1)}, bf16[1,1024,512]{2,1,0:T(8,128)(2,1)}, u32[]{:S(2)}) copy-start(bf16[1,1024,512]{2,1,0:T(8,128)(2,1)} %param.15) | copy-start | bytes 3145732
  259.5 1088.8 %copy-start.14 = (bf16[1,512,1024]{2,1,0:T(8,128)(2,1)S(1)}, bf16[1,512,1024]{2,1,0:T(8,128)(2,1)}, u32[]{:S(2)}) copy-start(bf16[1,512,1024]{2,1,0:T(8,128)(2,1)} %param.17) | copy-start | bytes 3145732
  259.5 1088.8 %all-to-all-start = ((bf16[32,1289,1024]{2,1,0:T(8,128)(2,1)}), bf16[32,1289,1024]{2,1,0:T(8,128)(2,1)}, u32[]{:S(2)}, u32[]{:S(2)}) async-start(bf16[32,1289,1024]{2,1,0:T(8,128)(2,1)} %pad_maximum_fusion), calls=%async_computation | async-start | bytes 169869312 | tf_op jit(solution)/shard_map/all_to_all | solution.py:58
  1478.6 141.9 %copy-start.11 = (f32[1024,8]{0,1:T(8,128)S(1)}, f32[1024,8]{0,1:T(8,128)}, u32[]{:S(2)}) copy-start(f32[1024,8]{0,1:T(8,128)} %param.12) | copy-start | bytes 98308
  1478.6 146.8 %copy-start.3 = (s32[8192]{0:T(1024)S(1)}, s32[8192]{0:T(1024)}, u32[]{:S(2)}) copy-start(s32[8192]{0:T(1024)} %copy-done.2) | copy-start | bytes 98308
  1478.6 177.3 %copy-start.6 = (s32[32]{0:T(128)S(1)}, s32[32]{0:T(128)}, u32[]{:S(2)}) copy-start(s32[32]{0:T(128)} %copy-done.5) | copy-start | bytes 388
  1478.6 178.8 %copy-start.8 = (s32[8192,1]{0,1:T(1,128)S(1)}, s32[8192,1]{0,1:T(1,128)}, u32[]{:S(2)}) copy-start(s32[8192,1]{0,1:T(1,128)} %copy-done.7) | copy-start | bytes 98308
  1478.6 185.8 %copy-start.10 = (s32[8192]{0:T(1024)S(1)}, s32[8192]{0:T(1024)}, u32[]{:S(2)}) copy-start(s32[8192]{0:T(1024)} %copy-done.9) | copy-start | bytes 98308
  1478.6 1220.3 %all-to-all-start.1 = ((bf16[32,1289,1024]{2,1,0:T(8,128)(2,1)}), bf16[32,1289,1024]{2,1,0:T(8,128)(2,1)}, u32[]{:S(2)}, u32[]{:S(2)}) async-start(bf16[32,1289,1024]{2,1,0:T(8,128)(2,1)} %pad_maximum_fusion.1), calls=%async_computation.1 | async-start | bytes 169869312 | tf_op jit(solution)/shard_map/all_to_all | solution.py:68
  2816.3 48.9 %copy-start.1 = (bf16[1024,1024]{1,0:T(8,128)(2,1)S(1)}, bf16[1024,1024]{1,0:T(8,128)(2,1)}, u32[]{:S(2)}) copy-start(bf16[1024,1024]{1,0:T(8,128)(2,1)} %param.10) | copy-start | bytes 6291460
where the time goes:
time: 2920 us; the launch traced here: 2870 us
  waiting for transfers between devices  2100 us (72%)
  local copies, waits for them, and re-layouts  307 us (11%)
  other arithmetic  262 us (9%)
  starting transfers between devices  133 us (5%)
  matrix products  56.5 us (2%)
    all_to_all x1, waiting for transfers between devices, local_layer(): recv_buf = lax.all_to_all(send_buf, 'ep', 0, 0, tiled=True)  1080 us
    all_to_all x1, waiting for transfers between devices, local_layer(): ret_buf = lax.all_to_all(back_buf, 'ep', 0, 0, tiled=True)  1020 us
    all_to_all x1, starting transfers between devices, local_layer(): ret_buf = lax.all_to_all(back_buf, 'ep', 0, 0, tiled=True)  125 us
    gather x2, local copies, waits for them, and re-layouts, combine_rows(): picked = out_rows[all_slots]  88.7 us
  transfers between devices with their start and end apart: 2, of which 2 were waited for; matrix products, arithmetic and copies ran while one was open for 3% of the time, Pallas kernels for 0%

commit v1 on v0

v1 whole, which is shorter than its diff:
```python
import functools

import jax
import jax.numpy as jnp
from jax import lax
from jax.experimental import pallas as pl
from jax.experimental.pallas import tpu as pltpu
from jax.sharding import PartitionSpec as P

MESH = pl.DeviceIdType.MESH
F32 = jnp.float32
BF16 = jnp.bfloat16
OFFSETS = ((0, 0), (1, 1), (3, 3), (1, 3), (3, 1), (2, 2), (1, 2), (3, 2), (2, 1), (2, 3),
           (1, 0), (3, 0), (0, 1), (0, 3), (2, 0), (0, 2))
SIDE = 4
HOT_STEP = 16
LAG = 2


def packed(values):
    return sum(v << (2 * i) for i, v in enumerate(values[1:]))


TABLE_X = packed([o[0] for o in OFFSETS])
TABLE_Y = packed([o[1] for o in OFFSETS])


def moe_kernel(n, cap_p, x_ref, ids_ref, gates_ref, hot_tok_ref, hot_g_ref, wg_ref, wu_ref, wd_ref, out_ref,
               own, hot, xbuf, hbuf, slot_t, gate_t, slot_r, hot_w, acc,
               w_sem, s1_send, s1_recv, s2_send, s2_recv, s3_send, s3_recv,
               x_send, x_recv, h_send, h_recv, free):
    tokens, d_model = x_ref.shape
    top_k = ids_ref.shape[1]
    d_ff = wg_ref.shape[2]
    lanes = slot_t.shape[1]
    chunk = own.shape[0] // n
    half = n // 2
    me = lax.axis_index('ep')
    core = lax.rem(me, 2)
    chip = lax.div(me, 2)
    px = lax.rem(chip, SIDE)
    py = lax.div(chip, SIDE)

    barrier = pltpu.get_barrier_semaphore()

    def greet(k, c):
        pl.semaphore_signal(barrier, inc=1, device_id={'ep': lax.rem(me + k, n)}, device_id_type=MESH)
        return c
    lax.fori_loop(1, n, greet, 0)

    w_copies = (
        pltpu.make_async_copy(wg_ref.at[0], own.at[pl.ds(0, d_model), pl.ds(0, d_ff)], w_sem.at[0]),
        pltpu.make_async_copy(wu_ref.at[0], own.at[pl.ds(0, d_model), pl.ds(d_ff, d_ff)], w_sem.at[1]),
        pltpu.make_async_copy(wd_ref.at[0], own.at[pl.ds(d_model, d_ff), :], w_sem.at[2]),
    )
    for copy in w_copies:
        copy.start()

    def shifted(q, sign):
        j = lax.div(q, 2)
        i = 2 * lax.max(j - 1, 0)
        near = lax.min(j, 1)
        dx = lax.rem(lax.shift_right_logical(jnp.int32(TABLE_X), i), SIDE) * near
        dy = lax.rem(lax.shift_right_logical(jnp.int32(TABLE_Y), i), SIDE) * near
        dc = lax.rem(q, 2)
        tx = lax.rem(px + sign * dx + SIDE, SIDE)
        ty = lax.rem(py + sign * dy + SIDE, SIDE)
        return (ty * SIDE + tx) * 2 + lax.rem(core + dc, 2)

    def x_copy(q):
        return pltpu.make_async_remote_copy(
            src_ref=xbuf.at[q], dst_ref=hbuf.at[q], send_sem=x_send.at[q], recv_sem=x_recv.at[q],
            device_id={'ep': shifted(q, 1)}, device_id_type=MESH)

    def h_copy(q):
        return pltpu.make_async_remote_copy(
            src_ref=hbuf.at[q], dst_ref=xbuf.at[q], send_sem=h_send.at[q], recv_sem=h_recv.at[q],
            device_id={'ep': shifted(q, -1)}, device_id_type=MESH)

    lane = lax.broadcasted_iota(jnp.int32, (tokens, lanes), 1)
    chosen = jnp.zeros((tokens, lanes), F32)
    gate_sum = jnp.zeros((tokens, lanes), F32)
    for j in range(top_k):
        hit = ids_ref[:, j:j + 1] == lane
        chosen = jnp.where(hit, 1.0, chosen)
        gate_sum = jnp.where(hit, gates_ref[:, j:j + 1], gate_sum)
    gate_t[...] = gate_sum
    chosen_b = chosen.astype(BF16)
    step = 256
    for r in range(tokens // step):
        rows = lax.broadcasted_iota(jnp.int32, (step, tokens), 0) + r * step
        before = jnp.where(lax.broadcasted_iota(jnp.int32, (step, tokens), 1) < rows, 1.0, 0.0).astype(BF16)
        rank = jnp.dot(before, chosen_b, preferred_element_type=F32)
        slot_t[pl.ds(r * step, step), :] = jnp.where(chosen[r * step:(r + 1) * step] > 0.5, rank, -1.0)
    slot_r[...] = slot_t[...].T

    pl.semaphore_wait(barrier, n - 1)

    for copy in w_copies:
        copy.wait()

    def piece(d):
        return pl.ds(pl.multiple_of((lax.rem(d, 2) * half + lax.div(d, 2)) * chunk, chunk), chunk)

    def s1_copy(d):
        return pltpu.make_async_remote_copy(
            src_ref=own.at[piece(d), :], dst_ref=hot.at[piece(d), :], send_sem=s1_send.at[d], recv_sem=s1_recv,
            device_id={'ep': d}, device_id_type=MESH)

    @pl.when(me == 0)
    def _():
        hot[pl.ds(0, chunk), :] = own[pl.ds(0, chunk), :]

        def send(d, c):
            s1_copy(d).start()
            return c
        lax.fori_loop(1, n, send, 0)

    def s2_copy(k):
        peer = lax.rem(chip + k, half) * 2 + core
        return pltpu.make_async_remote_copy(
            src_ref=hot.at[piece(me), :], dst_ref=hot.at[piece(me), :], send_sem=s2_send.at[k], recv_sem=s2_recv.at[k],
            device_id={'ep': peer}, device_id_type=MESH)

    def s2_arrival(k):
        peer = lax.rem(chip + half - k, half) * 2 + core
        return pltpu.make_async_remote_copy(
            src_ref=hot.at[piece(peer), :], dst_ref=hot.at[piece(peer), :], send_sem=s2_send.at[k],
            recv_sem=s2_recv.at[k], device_id={'ep': peer}, device_id_type=MESH)

    def core_half(c):
        return hot.at[pl.ds(pl.multiple_of(c * half * chunk, chunk), half * chunk), :]

    def s3_copy(c):
        return pltpu.make_async_remote_copy(
            src_ref=core_half(c), dst_ref=core_half(c), send_sem=s3_send, recv_sem=s3_recv,
            device_id={'ep': chip * 2 + 1 - core}, device_id_type=MESH)

    def gather(q):
        place = slot_r[pl.ds(shifted(q, 1), 1), :]
        pos = lax.broadcasted_iota(jnp.int32, (cap_p, tokens), 0).astype(F32)
        pick = jnp.where(pos == place, 1.0, 0.0).astype(BF16)
        return jnp.dot(pick, x_ref[...], preferred_element_type=F32).astype(BF16)

    def gather_step(q, c):
        xbuf[q] = gather(q)

        @pl.when(q >= 2)
        def _():
            x_copy(q - 1).start()
        return c
    lax.fori_loop(1, n, gather_step, 0)
    hbuf[0] = gather(0)
    x_copy(n - 1).start()

    @pl.when(me != 0)
    def _():
        s1_copy(me).wait_recv()

    def s2_send_step(k, c):
        s2_copy(k).start()
        return c
    lax.fori_loop(1, half, s2_send_step, 0)

    def swiglu(rows, weights):
        mid = jnp.dot(rows, weights[pl.ds(0, d_model), :], preferred_element_type=F32)
        a = mid[:, :d_ff]
        u = (a * jax.nn.sigmoid(a) * mid[:, d_ff:]).astype(BF16)
        return jnp.dot(u, weights[pl.ds(d_model, d_ff), :], preferred_element_type=F32).astype(BF16)

    def send_back(q):
        pl.semaphore_wait(free.at[q], 1)
        h_copy(q).start()

    def expert_step(q, c):
        @pl.when(q >= 1)
        def _():
            x_copy(q).wait()
            pl.semaphore_signal(free.at[q], inc=1, device_id={'ep': shifted(q, 1)}, device_id_type=MESH)
        hbuf[q] = swiglu(hbuf[q], own)

        @pl.when(q > LAG)
        def _():
            send_back(q - LAG)
        return c
    lax.fori_loop(0, n, expert_step, 0)
    for q in range(n - LAG, n):
        send_back(q)

    tile = 256
    tiles = tokens // tile
    own_lane = lax.broadcasted_iota(jnp.int32, (tile, lanes), 1)
    pos_lane = lax.broadcasted_iota(jnp.int32, (tile, cap_p), 1).astype(F32)

    def combine(e, rows):
        def body(i, c):
            at = pl.ds(pl.multiple_of(i * tile, tile), tile)
            mine = own_lane == e
            place = jnp.sum(jnp.where(mine, slot_t[at, :], 0.0), axis=1, keepdims=True)
            gate = jnp.sum(jnp.where(mine, gate_t[at, :], 0.0), axis=1, keepdims=True)
            pick = jnp.where(pos_lane == place, 1.0, 0.0).astype(BF16)
            acc[at, :] += gate * jnp.dot(pick, rows[...], preferred_element_type=F32)
            return c
        lax.fori_loop(0, tiles, body, 0)

    def hot_gate(i, c):
        at = pl.ds(pl.multiple_of(i * tile, tile), tile)
        tok = lax.broadcasted_iota(jnp.int32, (tile, hot_tok_ref.shape[1]), 0) + i * tile
        hot_w[at, :] = jnp.sum(jnp.where(hot_tok_ref[...] == tok, hot_g_ref[...], 0.0), axis=1, keepdims=True)
        acc[at, :] = jnp.zeros((tile, d_model), F32)
        return c
    lax.fori_loop(0, tiles, hot_gate, 0)
    combine(me, hbuf.at[0])

    def combine_step(q, c):
        @pl.when(q == HOT_STEP - 4)
        def _():
            def arrived(k, c):
                s2_arrival(k).wait_recv()
                s2_copy(k).wait_send()
                return c
            lax.fori_loop(1, half, arrived, 0)
            s3_copy(core).start()

        @pl.when(q == HOT_STEP)
        def _():
            s3_copy(core).wait_send()
            s3_copy(1 - core).wait_recv()

            def hot_step(i, c):
                at = pl.ds(pl.multiple_of(i * tile, tile), tile)
                acc[at, :] += hot_w[at, :] * swiglu(x_ref[at, :], hot).astype(F32)
                return c
            lax.fori_loop(0, tiles, hot_step, 0)

        h_copy(q).wait()
        combine(shifted(q, 1), xbuf.at[q])
        return c
    lax.fori_loop(1, n, combine_step, 0)

    @pl.when(me == 0)
    def _():
        def sent(d, c):
            s1_copy(d).wait_send()
            return c
        lax.fori_loop(1, n, sent, 0)

    def store(i, c):
        at = pl.ds(pl.multiple_of(i * tile, tile), tile)
        out_ref[at, :] = acc[at, :].astype(BF16)
        return c
    lax.fori_loop(0, tiles, store, 0)


def solution(mesh):
    n = mesh.shape['ep']
    row_spec = P(('dp', 'ep'), None)
    list_spec = P(('dp', 'ep'))
    expert_spec = P('ep', None, None)

    def local_layer(x, ids, gates, hot_tok, hot_g, wg, wu, wd):
        tokens, d_model = x.shape
        top_k = ids.shape[1]
        d_ff = wg.shape[2]
        cap = (tokens * top_k + n - 2) // (n - 1)
        cap_p = -(-cap // 16) * 16
        lanes = -(-n // 128) * 128
        half = n // 2
        vmem = pl.BlockSpec(memory_space=pltpu.VMEM)
        hbm = pl.BlockSpec(memory_space=pltpu.HBM)
        dma = pltpu.SemaphoreType.DMA
        return pl.pallas_call(
            functools.partial(moe_kernel, n, cap_p),
            out_shape=jax.ShapeDtypeStruct((tokens, d_model), BF16),
            in_specs=[vmem] * 5 + [hbm] * 3,
            out_specs=vmem,
            scratch_shapes=[
                pltpu.VMEM((d_model + d_ff, d_model), BF16),
                pltpu.VMEM((d_model + d_ff, d_model), BF16),
                pltpu.VMEM((n, cap_p, d_model), BF16),
                pltpu.VMEM((n, cap_p, d_model), BF16),
                pltpu.VMEM((tokens, lanes), F32),
                pltpu.VMEM((tokens, lanes), F32),
                pltpu.VMEM((lanes, tokens), F32),
                pltpu.VMEM((tokens, 1), F32),
                pltpu.VMEM((tokens, d_model), F32),
                dma((3,)), dma((n,)), dma, dma((half,)), dma((half,)), dma, dma,
                dma((n,)), dma((n,)), dma((n,)), dma((n,)),
                pltpu.SemaphoreType.REGULAR((n,)),
            ],
            compiler_params=pltpu.CompilerParams(
                collective_id=0, has_side_effects=True, vmem_limit_bytes=67_043_328),
        )(x, ids, gates, hot_tok.reshape(1, -1), hot_g.reshape(1, -1), wg, wu, wd)

    return jax.shard_map(local_layer, mesh=mesh,
                         in_specs=(row_spec, row_spec, row_spec, list_spec, list_spec, expert_spec, expert_spec, expert_spec),
                         out_specs=row_spec, check_vma=False)
```

time: 2920 us -> 579 us (0.20); the launches traced: 2870 us -> 572 us
  waiting for transfers between devices: 2100 us -> 0 us
  Pallas kernels: 0 us -> 565 us
  local copies, waits for them, and re-layouts: 307 us -> 6.6 us
  other arithmetic: 262 us -> 0 us
  starting transfers between devices: 133 us -> 0 us
  matrix products: 56.5 us -> 0 us
    all_to_all x2 -> x0, waiting for transfers between devices: 2100 us -> none  [the longest x1 1080 us: local_layer(): recv_buf = lax.all_to_all(send_buf, 'ep', 0, 0, tiled=True)]
    pallas_call x0 -> x1, Pallas kernels: none -> 565 us  [local_layer(): pl.pallas_call(functools.partial(moe_kernel, n, cap_p), out_shape=jax.Sha...]
    gather x9 -> x0, local copies, waits for them, and re-layouts: 189 us -> none  [the longest x2 88.7 us: combine_rows(): picked = out_rows[all_slots]]
    concatenate x4 -> x0, other arithmetic: 137 us -> none  [the longest x1 57.1 us: local_layer(): jnp.concatenate([cold_out.reshape(group_size, block_rows, d_model), hot_o...]
    all_to_all x2 -> x0, starting transfers between devices: 133 us -> none  [the longest x1 125 us: local_layer(): ret_buf = lax.all_to_all(back_buf, 'ep', 0, 0, tiled=True)]
    scatter-add x1 -> x0, other arithmetic: 57 us -> none  [route_plan(): exp_counts = jnp.bincount(flat_ids, length=num_experts).astype(jnp.int32)]
    dot_general x3 -> x0, matrix products: 56.5 us -> none  [the longest x1 27.1 us: local_layer(): jnp.einsum('slcf,lfd->slcd', hidden, wd_loc, preferred_element_type=jnp.f...]
    scatter x3 -> x0, local copies, waits for them, and re-layouts: 51.3 us -> none  [the longest x1 30.5 us: route_plan(): jnp.zeros((routes,), jnp.int32).at[sort_order]]
  transfers between devices with their start and end apart: 2 -> 0, of which waited for: 2 -> 0; matrix products, arithmetic and copies ran while one was open for 3% -> 0% of each run, Pallas kernels for 0% -> 0%
where the time goes in v1:
time: 579 us; the launch traced here: 572 us
  Pallas kernels  565 us (98%)
  local copies, waits for them, and re-layouts  6.6 us (1%)
    pallas_call x1, Pallas kernels, local_layer(): pl.pallas_call(functools.partial(moe_kernel, n, cap_p), out_shape=jax.Sha...  565 us

profile of v1, /device:TPU:106, one launch (start us, length us, event | category | flops | bytes accessed | tf_op | source)
XLA Modules:
  0.0 571.7 jit_solution(3620821290531151646)
XLA Ops:
  0.0 1.8 copy.9.ids_ref
  1.8 1.8 copy.10.gates_ref
  3.5 565.1 %shard_map.82 = bf16[1024,1024]{1,0:T(8,128)(2,1)} custom-call(bf16[1024,1024]{1,0:T(8,128)(2,1)} %x_ref.1, s32[1024,8]{1,0:T(8,128)} %copy.9.ids_ref, f32[1024,8]{1,0:T(8,128)} %copy.10.gates_ref, s32[1,1024]{1,0:T(1,128)} %bitcast.2, f32[1,1024]{1,0:T(1,128)} %bitcast.3, bf16[1,1024,512]{2,1,0:T(8,128)(2,1)} %wg_ref.1, bf16[1,1024,512]{2,1,0:T(8,128)(2,1)} %wu_ref.1, ...), custom_call_target="tpu_custom_call" | custom-call | tf_op jit(solution)/shard_map/pallas_call | solution.py:272
  568.6 3.1 copy.12

commit v2 on v1

v2 whole, which is shorter than its diff:
```python
import functools

import jax
import jax.numpy as jnp
from jax import lax
from jax.experimental import pallas as pl
from jax.experimental.pallas import tpu as pltpu
from jax.sharding import PartitionSpec as P

MESH = pl.DeviceIdType.MESH
F32 = jnp.float32
BF16 = jnp.bfloat16
OFFSETS = ((0, 0), (1, 1), (3, 3), (1, 3), (3, 1), (2, 2), (1, 2), (3, 2), (2, 1), (2, 3),
           (1, 0), (3, 0), (0, 1), (0, 3), (2, 0), (0, 2))
SIDE = 4
RING = (0, 1, 3, 2)
ARRIVALS = tuple(sorted(OFFSETS, key=lambda o: max(RING.index(o[0]), RING.index(o[1]))))
EARLY = 16
HOT_SHARE = 18
HOT_RUN = 24


def packed(values):
    return sum(v << (2 * i) for i, v in enumerate(values))


def entry(table, i):
    return lax.rem(lax.shift_right_logical(jnp.int32(table), 2 * i), SIDE)


def place_of(order, t):
    j = lax.div(t, 2)
    i = lax.max(j - 1, 0)
    near = lax.min(j, 1)
    dx = entry(packed([o[0] for o in order[1:]]), i) * near
    dy = entry(packed([o[1] for o in order[1:]]), i) * near
    return dx, dy, lax.rem(t, 2)


def moe_kernel(n, cap_p, x_ref, ids_ref, gates_ref, hot_tok_ref, hot_g_ref, wg_ref, wu_ref, wd_ref, out_ref,
               own, hot, xbuf, hbuf, ring_x, ring_y, tab_x, tab_y, slot_t, gate_t, slot_r, slot_x, hot_w, acc,
               w_sem, s1_send, s1_recv, s2_send, s2_recv, s3_send, s3_recv,
               rows_send, rows_recv, tabs_send, tabs_recv, part_send, part_recv, h_send, h_recv, out_sem, free):
    tokens, d_model = x_ref.shape
    top_k = ids_ref.shape[0]
    d_ff = wg_ref.shape[2]
    lanes = slot_t.shape[1]
    chunk = own.shape[0] // n
    half = n // 2
    wide = d_model // 2
    me = lax.axis_index('ep')
    core = lax.rem(me, 2)
    chip = lax.div(me, 2)
    px = lax.rem(chip, SIDE)
    py = lax.div(chip, SIDE)

    def dev(dx, dy, dc):
        tx = lax.rem(px + dx + SIDE, SIDE)
        ty = lax.rem(py + dy + SIDE, SIDE)
        return (ty * SIDE + tx) * 2 + lax.rem(core + dc, 2)

    def slot_of(dx, dy, dc):
        return (dy * SIDE + dx) * 2 + dc

    def remote(src, dst, send, recv, device):
        return pltpu.make_async_remote_copy(src_ref=src, dst_ref=dst, send_sem=send, recv_sem=recv,
                                            device_id={'ep': device}, device_id_type=MESH)

    barrier = pltpu.get_barrier_semaphore()

    def greet(k, c):
        pl.semaphore_signal(barrier, inc=1, device_id={'ep': lax.rem(me + k, n)}, device_id_type=MESH)
        return c
    lax.fori_loop(1, n, greet, 0)

    w_copies = (
        pltpu.make_async_copy(wg_ref.at[0], own.at[pl.ds(0, d_model), pl.ds(0, d_ff)], w_sem.at[0]),
        pltpu.make_async_copy(wu_ref.at[0], own.at[pl.ds(0, d_model), pl.ds(d_ff, d_ff)], w_sem.at[1]),
        pltpu.make_async_copy(wd_ref.at[0], own.at[pl.ds(d_model, d_ff), :], w_sem.at[2]),
    )
    for copy in w_copies:
        copy.start()
    pl.semaphore_wait(barrier, n - 1)

    cols = (pl.ds(0, wide), pl.ds(wide, wide))
    rings = (ring_x, ring_y)
    tabs = (tab_x, tab_y)

    def step_of(axis, a):
        return dev(a, 0, 0) if axis == 0 else dev(0, a, 0)

    def rows_copy(axis, a):
        return remote(x_ref.at[:, cols[axis]], rings[axis].at[a - 1], rows_send.at[axis, a], rows_recv.at[axis, a],
                      step_of(axis, a))

    def tabs_copy(axis, a):
        if axis == 0:
            src = slot_x.at[pl.ds(pl.multiple_of(lax.rem(px + a, SIDE) * 8, 8), 8), :]
        else:
            src = slot_r.at[pl.ds(pl.multiple_of(lax.rem(py + a, SIDE) * 8, 8), 8), :]
        return remote(src, tabs[axis].at[a], tabs_send.at[axis, a], tabs_recv.at[axis, a], step_of(axis, a))

    for a in RING[1:]:
        for axis in (0, 1):
            rows_copy(axis, a).start()

    expert = lax.broadcasted_iota(jnp.int32, (lanes, tokens), 0)
    chosen = jnp.zeros((lanes, tokens), F32)
    gate_sum = jnp.zeros((lanes, tokens), F32)
    for j in range(top_k):
        hit = ids_ref[pl.ds(j, 1), :] == expert
        chosen = jnp.where(hit, 1.0, chosen)
        gate_sum = jnp.where(hit, gates_ref[pl.ds(j, 1), :], gate_sum)
    gate_t[...] = gate_sum.T
    chosen_b = chosen.astype(BF16)
    step = 256
    for r in range(tokens // step):
        upto = lax.broadcasted_iota(jnp.int32, (tokens, step), 1) + r * step
        before = jnp.where(lax.broadcasted_iota(jnp.int32, (tokens, step), 0) < upto, 1.0, 0.0).astype(BF16)
        rank = jnp.dot(chosen_b, before, preferred_element_type=F32)
        slot_r[:, pl.ds(r * step, step)] = jnp.where(chosen[:, r * step:(r + 1) * step] > 0.5, rank, -1.0)
    slot_t[...] = slot_r[...].T
    for tx in range(SIDE):
        for ty in range(SIDE):
            slot_x[pl.ds(tx * 8 + ty * 2, 2), :] = slot_r[pl.ds((ty * SIDE + tx) * 2, 2), :]
    tab_x[0] = slot_x[pl.ds(pl.multiple_of(px * 8, 8), 8), :]
    tab_y[0] = slot_r[pl.ds(pl.multiple_of(py * 8, 8), 8), :]
    for a in RING[1:]:
        for axis in (0, 1):
            tabs_copy(axis, a).start()

    def part(axis, a, m):
        b = entry(packed(RING[1:] + RING[:1]), lax.div(m, 2))
        dc = lax.rem(m, 2)
        q = slot_of(a, b, dc) if axis == 0 else slot_of(b, a, dc)
        target = dev(0, b, dc) if axis == 0 else dev(b, 0, dc)
        row = lax.rem((py if axis == 0 else px) + b, SIDE) * 2 + lax.rem(core + dc, 2)
        return q, target, row

    def part_copy(axis, q, target):
        return remote(xbuf.at[q, :, cols[axis]], hbuf.at[q, :, cols[axis]], part_send.at[axis, q],
                      part_recv.at[axis, q], target)

    pos = lax.broadcasted_iota(jnp.int32, (cap_p, tokens), 0).astype(F32)

    def gather(axis, a, m):
        q, target, row = part(axis, a, m)

        @pl.when(target != 0)
        def _():
            source = x_ref[:, cols[axis]] if a == 0 else rings[axis][a - 1]
            pick = jnp.where(pos == tabs[axis][a, pl.ds(row, 1), :], 1.0, 0.0).astype(BF16)
            xbuf[q, :, cols[axis]] = jnp.dot(pick, source, preferred_element_type=F32).astype(BF16)

    def post(axis, a, m):
        q, target, row = part(axis, a, m)

        @pl.when((target != 0) & (target != me))
        def _():
            part_copy(axis, q, target).start()

        @pl.when((target != 0) & (target == me))
        def _():
            hbuf[q, :, cols[axis]] = xbuf[q, :, cols[axis]]

    for a in RING:
        if a:
            for axis in (0, 1):
                rows_copy(axis, a).wait_recv()
                tabs_copy(axis, a).wait_recv()

        def gather_step(m, c, a=a):
            gather(0, a, m)

            @pl.when(m > 0)
            def _():
                post(1, a, m - 1)
            gather(1, a, m)
            post(0, a, m)
            return c
        lax.fori_loop(0, 2 * SIDE, gather_step, 0)
        post(1, a, jnp.int32(2 * SIDE - 1))

    for a in RING[1:]:
        for axis in (0, 1):
            rows_copy(axis, a).wait_send()
            tabs_copy(axis, a).wait_send()
    for copy in w_copies:
        copy.wait()

    def swiglu(rows, weights):
        mid = jnp.dot(rows, weights[pl.ds(0, d_model), :], preferred_element_type=F32)
        a = mid[:, :d_ff]
        u = (a * jax.nn.sigmoid(a) * mid[:, d_ff:]).astype(BF16)
        return jnp.dot(u, weights[pl.ds(d_model, d_ff), :], preferred_element_type=F32).astype(BF16)

    def h_copy(dx, dy, dc):
        q = slot_of(dx, dy, dc)
        return remote(hbuf.at[q], xbuf.at[q], h_send.at[q], h_recv.at[q], dev(-dx, -dy, dc))

    def expert_step(t, c):
        dx, dy, dc = place_of(ARRIVALS, t)
        q = slot_of(dx, dy, dc)
        for axis, target in ((0, dev(0, dy, dc)), (1, dev(dx, 0, dc))):
            @pl.when((target != 0) & (target != me))
            def _():
                part_copy(axis, q, target).wait_send()
        maker = dev(dx, dy, dc)

        @pl.when((maker != 0) & (maker != me))
        def _():
            pl.semaphore_signal(free.at[q], inc=1, device_id={'ep': maker}, device_id_type=MESH)

        @pl.when(me != 0)
        def _():
            for axis, target in ((0, dev(0, dy, dc)), (1, dev(dx, 0, dc))):
                @pl.when(target != me)
                def _():
                    part_copy(axis, q, target).wait_recv()
            hbuf[q] = swiglu(hbuf[q], own)
        return c
    lax.fori_loop(0, n, expert_step, 0)

    def piece(d):
        return pl.ds(pl.multiple_of((lax.rem(d, 2) * half + lax.div(d, 2)) * chunk, chunk), chunk)

    def s1_copy(d):
        return remote(own.at[piece(d), :], hot.at[piece(d), :], s1_send.at[d], s1_recv, d)

    def s2_copy(j, sign=1):
        dx, dy, dc = place_of(OFFSETS, 2 * j)
        peer = dev(sign * dx, sign * dy, 0)
        held = piece(me if sign == 1 else peer)
        return remote(hot.at[held, :], hot.at[held, :], s2_send.at[j], s2_recv.at[j], peer)

    def core_half(c):
        return hot.at[pl.ds(pl.multiple_of(c * half * chunk, chunk), half * chunk), :]

    def s3_copy(c):
        return remote(core_half(c), core_half(c), s3_send, s3_recv, dev(0, 0, 1))

    @pl.when(me == 0)
    def _():
        hot[pl.ds(0, chunk), :] = own[pl.ds(0, chunk), :]

        def send(t, c):
            dx, dy, dc = place_of(OFFSETS, t)
            s1_copy(dev(dx, dy, dc)).start()
            return c
        lax.fori_loop(1, n, send, 0)

    def send_back(t, c):
        dx, dy, dc = place_of(OFFSETS, t)

        @pl.when(me != 0)
        def _():
            pl.semaphore_wait(free.at[slot_of(dx, dy, dc)], 1)
            h_copy(dx, dy, dc).start()
        return c
    lax.fori_loop(1, EARLY, send_back, 0)

    @pl.when(me != 0)
    def _():
        s1_copy(me).wait_recv()

    def s2_step(j, c):
        s2_copy(j).start()
        return c
    lax.fori_loop(1, half, s2_step, 0)
    lax.fori_loop(EARLY, n, send_back, 0)

    tile = 256
    tiles = tokens // tile
    own_lane = lax.broadcasted_iota(jnp.int32, (tile, lanes), 1)
    pos_lane = lax.broadcasted_iota(jnp.int32, (tile, cap_p), 1).astype(F32)

    def combine(e, rows):
        def body(i, c):
            at = pl.ds(pl.multiple_of(i * tile, tile), tile)
            mine = own_lane == e
            place = jnp.sum(jnp.where(mine, slot_t[at, :], 0.0), axis=1, keepdims=True)
            gate = jnp.sum(jnp.where(mine, gate_t[at, :], 0.0), axis=1, keepdims=True)
            pick = jnp.where(pos_lane == place, 1.0, 0.0).astype(BF16)
            acc[at, :] += gate * jnp.dot(pick, rows[...], preferred_element_type=F32)
            return c
        lax.fori_loop(0, tiles, body, 0)

    def hot_gate(i, c):
        at = pl.ds(pl.multiple_of(i * tile, tile), tile)
        tok = lax.broadcasted_iota(jnp.int32, (tile, hot_tok_ref.shape[1]), 0) + i * tile
        hot_w[at, :] = jnp.sum(jnp.where(hot_tok_ref[...] == tok, hot_g_ref[...], 0.0), axis=1, keepdims=True)
        acc[at, :] = jnp.zeros((tile, d_model), F32)
        return c
    lax.fori_loop(0, tiles, hot_gate, 0)

    @pl.when(me != 0)
    def _():
        combine(me, hbuf.at[0])

    def combine_step(t, c):
        @pl.when(t == HOT_SHARE)
        def _():
            def arrived(j, c):
                s2_copy(j, -1).wait_recv()
                s2_copy(j).wait_send()
                return c
            lax.fori_loop(1, half, arrived, 0)
            s3_copy(core).start()

        @pl.when(t == HOT_RUN)
        def _():
            s3_copy(core).wait_send()
            s3_copy(1 - core).wait_recv()

            def hot_step(i, c):
                at = pl.ds(pl.multiple_of(i * tile, tile), tile)
                acc[at, :] += hot_w[at, :] * swiglu(x_ref[at, :], hot).astype(F32)
                return c
            lax.fori_loop(0, tiles, hot_step, 0)

        dx, dy, dc = place_of(OFFSETS, t)
        maker = dev(dx, dy, dc)

        @pl.when(me != 0)
        def _():
            h_copy(dx, dy, dc).wait_send()

        @pl.when(maker != 0)
        def _():
            h_copy(dx, dy, dc).wait_recv()
            combine(maker, xbuf.at[slot_of(dx, dy, dc)])
        return c
    lax.fori_loop(1, n, combine_step, 0)

    @pl.when(me == 0)
    def _():
        def sent(d, c):
            s1_copy(d).wait_send()
            return c
        lax.fori_loop(1, n, sent, 0)

    def out_copy(axis, i):
        at = pl.ds(pl.multiple_of(i * tile, tile), tile)
        return pltpu.make_async_copy(rings[axis].at[0, at, :], out_ref.at[at, cols[axis]], out_sem.at[axis, i])

    for i in range(tiles):
        for axis in (0, 1):
            rings[axis][0, pl.ds(i * tile, tile), :] = acc[pl.ds(i * tile, tile), cols[axis]].astype(BF16)
            if i:
                out_copy(axis, i - 1).start()
    for axis in (0, 1):
        out_copy(axis, tiles - 1).start()
    for i in range(tiles):
        for axis in (0, 1):
            out_copy(axis, i).wait()


def solution(mesh):
    n = mesh.shape['ep']
    row_spec = P(('dp', 'ep'), None)
    list_spec = P(('dp', 'ep'))
    expert_spec = P('ep', None, None)

    def local_layer(x, ids, gates, hot_tok, hot_g, wg, wu, wd):
        tokens, d_model = x.shape
        top_k = ids.shape[1]
        d_ff = wg.shape[2]
        cap = (tokens * top_k + n - 2) // (n - 1)
        cap_p = -(-cap // 16) * 16
        lanes = -(-n // 128) * 128
        half = n // 2
        vmem = pl.BlockSpec(memory_space=pltpu.VMEM)
        hbm = pl.BlockSpec(memory_space=pltpu.HBM)
        dma = pltpu.SemaphoreType.DMA
        return pl.pallas_call(
            functools.partial(moe_kernel, n, cap_p),
            out_shape=jax.ShapeDtypeStruct((tokens, d_model), BF16),
            in_specs=[vmem] * 5 + [hbm] * 3,
            out_specs=hbm,
            scratch_shapes=[
                pltpu.VMEM((d_model + d_ff, d_model), BF16),
                pltpu.VMEM((d_model + d_ff, d_model), BF16),
                pltpu.VMEM((n, cap_p, d_model), BF16),
                pltpu.VMEM((n, cap_p, d_model), BF16),
                pltpu.VMEM((SIDE - 1, tokens, d_model // 2), BF16),
                pltpu.VMEM((SIDE - 1, tokens, d_model // 2), BF16),
                pltpu.VMEM((SIDE, 2 * SIDE, tokens), F32),
                pltpu.VMEM((SIDE, 2 * SIDE, tokens), F32),
                pltpu.VMEM((tokens, lanes), F32),
                pltpu.VMEM((tokens, lanes), F32),
                pltpu.VMEM((lanes, tokens), F32),
                pltpu.VMEM((n, tokens), F32),
                pltpu.VMEM((tokens, 1), F32),
                pltpu.VMEM((tokens, d_model), F32),
                dma((3,)), dma((n,)), dma, dma((half,)), dma((half,)), dma, dma,
                dma((2, SIDE)), dma((2, SIDE)), dma((2, SIDE)), dma((2, SIDE)),
                dma((2, n)), dma((2, n)), dma((n,)), dma((n,)), dma((2, tokens // 256)),
                pltpu.SemaphoreType.REGULAR((n,)),
            ],
            compiler_params=pltpu.CompilerParams(
                collective_id=0, has_side_effects=True, vmem_limit_bytes=67_043_328),
        )(x, ids.T, gates.T, hot_tok.reshape(1, -1), hot_g.reshape(1, -1), wg, wu, wd)

    return jax.shard_map(local_layer, mesh=mesh,
                         in_specs=(row_spec, row_spec, row_spec, list_spec, list_spec, expert_spec, expert_spec, expert_spec),
                         out_specs=row_spec, check_vma=False)
```

time: 579 us -> 460 us (0.79)
  the two profiles are of different devices: /device:TPU:106 before, /device:TPU:98 now
where the time goes in v2:
time: 460 us
  Pallas kernels  457 us (99%)
    pallas_call x1, Pallas kernels, local_layer(): pl.pallas_call(functools.partial(moe_kernel, n, cap_p), out_shape=jax.Sha...  457 us

profile of v2, /device:TPU:98, one launch (start us, length us, event | category | flops | bytes accessed | tf_op | source)
XLA Modules:
  0.0 460.1 jit_solution(8193696417631810068)
XLA Ops:
  0.0 457.0 %shard_map.82 = bf16[1024,1024]{1,0:T(8,128)(2,1)} custom-call(bf16[1024,1024]{1,0:T(8,128)(2,1)} %x_ref.1, s32[8,1024]{1,0:T(8,128)} %bitcast.4, f32[8,1024]{1,0:T(8,128)} %bitcast.5, s32[1,1024]{1,0:T(1,128)} %bitcast.6, f32[1,1024]{1,0:T(1,128)} %bitcast.7, bf16[1,1024,512]{2,1,0:T(8,128)(2,1)} %wg_ref.1, bf16[1,1024,512]{2,1,0:T(8,128)(2,1)} %wu_ref.1, ...), custom_call_target="tpu_custom_call" | custom-call | tf_op jit(solution)/shard_map/pallas_call | solution.py:375
  457.0 3.1 copy.10

commit v3 on v2

--- a/solution.py
+++ b/solution.py
@@ -15,9 +15,9 @@
 SIDE = 4
 RING = (0, 1, 3, 2)
 ARRIVALS = tuple(sorted(OFFSETS, key=lambda o: max(RING.index(o[0]), RING.index(o[1]))))
-EARLY = 16
-HOT_SHARE = 18
-HOT_RUN = 24
+HOT_LEG = 12
+HOT_SHARE = 10
+HOT_RUN = 16
 
 
 def packed(values):
@@ -40,7 +40,7 @@
 def moe_kernel(n, cap_p, x_ref, ids_ref, gates_ref, hot_tok_ref, hot_g_ref, wg_ref, wu_ref, wd_ref, out_ref,
                own, hot, xbuf, hbuf, ring_x, ring_y, tab_x, tab_y, slot_t, gate_t, slot_r, slot_x, hot_w, acc,
                w_sem, s1_send, s1_recv, s2_send, s2_recv, s3_send, s3_recv,
-               rows_send, rows_recv, tabs_send, tabs_recv, part_send, part_recv, h_send, h_recv, out_sem, free):
+               rows_send, rows_recv, tabs_send, tabs_recv, part_send, part_recv, h1_send, h1_recv, h2_send, h2_recv, out_sem, free, ready):
     tokens, d_model = x_ref.shape
     top_k = ids_ref.shape[0]
     d_ff = wg_ref.shape[2]
@@ -194,32 +194,61 @@
         u = (a * jax.nn.sigmoid(a) * mid[:, d_ff:]).astype(BF16)
         return jnp.dot(u, weights[pl.ds(d_model, d_ff), :], preferred_element_type=F32).astype(BF16)
 
-    def h_copy(dx, dy, dc):
-        q = slot_of(dx, dy, dc)
-        return remote(hbuf.at[q], xbuf.at[q], h_send.at[q], h_recv.at[q], dev(-dx, -dy, dc))
+    def back1(axis, dx, dy, dc):
+        q = slot_of(dx, dy, dc)
+        relay = dev(0, -dy, dc) if axis == 0 else dev(-dx, 0, dc)
+        return relay, remote(hbuf.at[q, :, cols[axis]], xbuf.at[q, :, cols[axis]], h1_send.at[axis, q],
+                             h1_recv.at[axis, q], relay)
+
+    def back2(axis, dx, dy, dc):
+        q = slot_of(dx, dy, dc)
+        source = dev(-dx, 0, 0) if axis == 0 else dev(0, -dy, 0)
+        return remote(xbuf.at[q, :, cols[axis]], hbuf.at[q, :, cols[axis]], h2_send.at[axis, q],
+                      h2_recv.at[axis, q], source)
+
+    def across(axis, dx, dy, dc):
+        return (dev(0, dy, dc), dx) if axis == 0 else (dev(dx, 0, dc), dy)
+
+    def send_back(t):
+        dx, dy, dc = place_of(ARRIVALS, t)
+        q = slot_of(dx, dy, dc)
+        for axis in (0, 1):
+            relay, copy = back1(axis, dx, dy, dc)
+
+            @pl.when((me != 0) & (relay != me))
+            def _():
+                pl.semaphore_wait(free.at[axis, q], 1)
+                copy.start()
+
+            @pl.when((me != 0) & (relay == me))
+            def _():
+                xbuf[q, :, cols[axis]] = hbuf[q, :, cols[axis]]
 
     def expert_step(t, c):
         dx, dy, dc = place_of(ARRIVALS, t)
         q = slot_of(dx, dy, dc)
-        for axis, target in ((0, dev(0, dy, dc)), (1, dev(dx, 0, dc))):
+        for axis in (0, 1):
+            target, _ = across(axis, dx, dy, dc)
+
             @pl.when((target != 0) & (target != me))
             def _():
                 part_copy(axis, q, target).wait_send()
-        maker = dev(dx, dy, dc)
-
-        @pl.when((maker != 0) & (maker != me))
-        def _():
-            pl.semaphore_signal(free.at[q], inc=1, device_id={'ep': maker}, device_id_type=MESH)
+                pl.semaphore_signal(free.at[axis, q], inc=1, device_id={'ep': target}, device_id_type=MESH)
 
         @pl.when(me != 0)
         def _():
-            for axis, target in ((0, dev(0, dy, dc)), (1, dev(dx, 0, dc))):
+            for axis in (0, 1):
+                target, _ = across(axis, dx, dy, dc)
+
                 @pl.when(target != me)
                 def _():
                     part_copy(axis, q, target).wait_recv()
             hbuf[q] = swiglu(hbuf[q], own)
+
+        @pl.when(t > 1)
+        def _():
+            send_back(t - 1)
         return c
-    lax.fori_loop(0, n, expert_step, 0)
 
     def piece(d):
         return pl.ds(pl.multiple_of((lax.rem(d, 2) * half + lax.div(d, 2)) * chunk, chunk), chunk)
@@ -227,11 +256,22 @@
     def s1_copy(d):
         return remote(own.at[piece(d), :], hot.at[piece(d), :], s1_send.at[d], s1_recv, d)
 
-    def s2_copy(j, sign=1):
-        dx, dy, dc = place_of(OFFSETS, 2 * j)
-        peer = dev(sign * dx, sign * dy, 0)
-        held = piece(me if sign == 1 else peer)
-        return remote(hot.at[held, :], hot.at[held, :], s2_send.at[j], s2_recv.at[j], peer)
+    def s2_copy(axis, a, b, arriving=False):
+        first = a is None
+        if first:
+            peer = step_of(axis, -b if arriving else b)
+            held = piece(peer if arriving else me)
+            i = b - 1
+        else:
+            back = b if arriving else 0
+            held = piece(dev(-a, -back, 0) if axis == 0 else dev(-back, -a, 0))
+            peer = step_of(1 - axis, -b if arriving else b)
+            i = SIDE - 1 + a * (SIDE - 1) + b - 1
+        at = hot.at[held, cols[axis]]
+        return remote(at, at, s2_send.at[axis, i], s2_recv.at[axis, i], peer)
+
+    LEG1 = [(axis, None, b) for b in RING[1:] for axis in (0, 1)]
+    LEG2 = [(axis, a, b) for a in RING for b in RING[1:] for axis in (0, 1)]
 
     def core_half(c):
         return hot.at[pl.ds(pl.multiple_of(c * half * chunk, chunk), half * chunk), :]
@@ -249,25 +289,59 @@
             return c
         lax.fori_loop(1, n, send, 0)
 
-    def send_back(t, c):
-        dx, dy, dc = place_of(OFFSETS, t)
-
-        @pl.when(me != 0)
-        def _():
-            pl.semaphore_wait(free.at[slot_of(dx, dy, dc)], 1)
-            h_copy(dx, dy, dc).start()
-        return c
-    lax.fori_loop(1, EARLY, send_back, 0)
+    lax.fori_loop(0, n, expert_step, 0)
+    send_back(jnp.int32(n - 1))
 
     @pl.when(me != 0)
     def _():
         s1_copy(me).wait_recv()
-
-    def s2_step(j, c):
-        s2_copy(j).start()
+    for leg in LEG1:
+        s2_copy(*leg).start()
+
+    def forward(t):
+        dx, dy, dc = place_of(ARRIVALS, t)
+        q = slot_of(dx, dy, dc)
+        for axis in (0, 1):
+            maker, steps = across(axis, dx, dy, dc)
+
+            @pl.when((maker != 0) & (maker != me))
+            def _():
+                back1(axis, dx, dy, dc)[1].wait_recv()
+
+            @pl.when((maker != 0) & (steps != 0))
+            def _():
+                pl.semaphore_wait(ready.at[axis, q], 1)
+                back2(axis, dx, dy, dc).start()
+
+    def relay_step(t, c):
+        @pl.when(t == HOT_LEG)
+        def _():
+            for leg in LEG1:
+                s2_copy(*leg, arriving=True).wait_recv()
+            for leg in LEG2:
+                s2_copy(*leg).start()
+
+        dx, dy, dc = place_of(ARRIVALS, t)
+        q = slot_of(dx, dy, dc)
+        for axis in (0, 1):
+            relay, copy = back1(axis, dx, dy, dc)
+
+            @pl.when((me != 0) & (relay != me))
+            def _():
+                copy.wait_send()
+            _, steps = across(axis, dx, dy, dc)
+            via = dev(dx, 0, 0) if axis == 0 else dev(0, dy, 0)
+
+            @pl.when((steps != 0) & (dev(dx, dy, dc) != 0))
+            def _():
+                pl.semaphore_signal(ready.at[axis, q], inc=1, device_id={'ep': via}, device_id_type=MESH)
+
+        @pl.when(t > 1)
+        def _():
+            forward(t - 1)
         return c
-    lax.fori_loop(1, half, s2_step, 0)
-    lax.fori_loop(EARLY, n, send_back, 0)
+    lax.fori_loop(1, n, relay_step, 0)
+    forward(jnp.int32(n - 1))
 
     tile = 256
     tiles = tokens // tile
@@ -300,11 +374,10 @@
     def combine_step(t, c):
         @pl.when(t == HOT_SHARE)
         def _():
-            def arrived(j, c):
-                s2_copy(j, -1).wait_recv()
-                s2_copy(j).wait_send()
-                return c
-            lax.fori_loop(1, half, arrived, 0)
+            for leg in LEG2:
+                s2_copy(*leg, arriving=True).wait_recv()
+            for leg in LEG1 + LEG2:
+                s2_copy(*leg).wait_send()
             s3_copy(core).start()
 
         @pl.when(t == HOT_RUN)
@@ -318,17 +391,29 @@
                 return c
             lax.fori_loop(0, tiles, hot_step, 0)
 
-        dx, dy, dc = place_of(OFFSETS, t)
+        dx, dy, dc = place_of(ARRIVALS, t)
+        q = slot_of(dx, dy, dc)
+        for axis in (0, 1):
+            through, steps = across(axis, dx, dy, dc)
+
+            @pl.when((through != 0) & (steps != 0))
+            def _():
+                back2(axis, dx, dy, dc).wait_send()
         maker = dev(dx, dy, dc)
 
-        @pl.when(me != 0)
-        def _():
-            h_copy(dx, dy, dc).wait_send()
-
         @pl.when(maker != 0)
         def _():
-            h_copy(dx, dy, dc).wait_recv()
-            combine(maker, xbuf.at[slot_of(dx, dy, dc)])
+            for axis in (0, 1):
+                _, steps = across(axis, dx, dy, dc)
+
+                @pl.when(steps != 0)
+                def _():
+                    back2(axis, dx, dy, dc).wait_recv()
+
+                @pl.when(steps == 0)
+                def _():
+                    hbuf[q, :, cols[axis]] = xbuf[q, :, cols[axis]]
+            combine(maker, hbuf.at[q])
         return c
     lax.fori_loop(1, n, combine_step, 0)
 
@@ -392,10 +477,10 @@
                 pltpu.VMEM((n, tokens), F32),
                 pltpu.VMEM((tokens, 1), F32),
                 pltpu.VMEM((tokens, d_model), F32),
-                dma((3,)), dma((n,)), dma, dma((half,)), dma((half,)), dma, dma,
+                dma((3,)), dma((n,)), dma, dma((2, half - 1)), dma((2, half - 1)), dma, dma,
                 dma((2, SIDE)), dma((2, SIDE)), dma((2, SIDE)), dma((2, SIDE)),
-                dma((2, n)), dma((2, n)), dma((n,)), dma((n,)), dma((2, tokens // 256)),
-                pltpu.SemaphoreType.REGULAR((n,)),
+                dma((2, n)), dma((2, n)), dma((2, n)), dma((2, n)), dma((2, n)), dma((2, n)), dma((2, tokens // 256)),
+                pltpu.SemaphoreType.REGULAR((2, n)), pltpu.SemaphoreType.REGULAR((2, n)),
             ],
             compiler_params=pltpu.CompilerParams(
                 collective_id=0, has_side_effects=True, vmem_limit_bytes=67_043_328),

time: 460 us -> 381 us (0.83)
  the two profiles are of different devices: /device:TPU:98 before, /device:TPU:106 now
where the time goes in v3:
time: 381 us; the launch traced here: 373 us
  Pallas kernels  370 us (97%)
    pallas_call x1, Pallas kernels, local_layer(): pl.pallas_call(functools.partial(moe_kernel, n, cap_p), out_shape=jax.Sha...  370 us

profile of v3, /device:TPU:106, one launch (start us, length us, event | category | flops | bytes accessed | tf_op | source)
XLA Modules:
  0.0 373.1 jit_solution(9889549283892921886)
XLA Ops:
  0.0 370.0 %shard_map.82 = bf16[1024,1024]{1,0:T(8,128)(2,1)} custom-call(bf16[1024,1024]{1,0:T(8,128)(2,1)} %x_ref.1, s32[8,1024]{1,0:T(8,128)} %bitcast.4, f32[8,1024]{1,0:T(8,128)} %bitcast.5, s32[1,1024]{1,0:T(1,128)} %bitcast.6, f32[1,1024]{1,0:T(1,128)} %bitcast.7, bf16[1,1024,512]{2,1,0:T(8,128)(2,1)} %wg_ref.1, bf16[1,1024,512]{2,1,0:T(8,128)(2,1)} %wu_ref.1, ...), custom_call_target="tpu_custom_call" | custom-call | tf_op jit(solution)/shard_map/pallas_call | solution.py:460
  370.0 3.1 copy.10

commit v4 on v3

--- a/solution.py
+++ b/solution.py
@@ -14,7 +14,7 @@
            (1, 0), (3, 0), (0, 1), (0, 3), (2, 0), (0, 2))
 SIDE = 4
 RING = (0, 1, 3, 2)
-ARRIVALS = tuple(sorted(OFFSETS, key=lambda o: max(RING.index(o[0]), RING.index(o[1]))))
+ARRIVALS = ((0, 0), (1, 0), (0, 1), (3, 0), (0, 3), (1, 1), (2, 0), (0, 2), (1, 3), (3, 1), (3, 3), (2, 1), (1, 2), (2, 3), (3, 2), (2, 2))
 HOT_LEG = 12
 HOT_SHARE = 10
 HOT_RUN = 16
@@ -100,7 +100,14 @@
             src = slot_r.at[pl.ds(pl.multiple_of(lax.rem(py + a, SIDE) * 8, 8), 8), :]
         return remote(src, tabs[axis].at[a], tabs_send.at[axis, a], tabs_recv.at[axis, a], step_of(axis, a))
 
-    for a in RING[1:]:
+    def rows_onward(axis, ahead):
+        at = pl.ds(0 if ahead else tokens // 2, tokens // 2)
+        ring = rings[axis]
+        i = 2 if ahead else 0
+        return remote(ring.at[0 if ahead else 2, at, :], ring.at[1, at, :], rows_send.at[axis, i],
+                      rows_recv.at[axis, i], step_of(axis, 1 if ahead else -1))
+
+    for a in (1, 3):
         for axis in (0, 1):
             rows_copy(axis, a).start()
 
@@ -164,9 +171,15 @@
             hbuf[q, :, cols[axis]] = xbuf[q, :, cols[axis]]
 
     for a in RING:
-        if a:
-            for axis in (0, 1):
-                rows_copy(axis, a).wait_recv()
+        for axis in (0, 1):
+            if a == 1:
+                for b in (1, 3):
+                    rows_copy(axis, b).wait_recv()
+                    rows_onward(axis, b == 1).start()
+            if a == 2:
+                for ahead in (True, False):
+                    rows_onward(axis, ahead).wait_recv()
+            if a:
                 tabs_copy(axis, a).wait_recv()
 
         def gather_step(m, c, a=a):
@@ -181,9 +194,11 @@
         lax.fori_loop(0, 2 * SIDE, gather_step, 0)
         post(1, a, jnp.int32(2 * SIDE - 1))
 
-    for a in RING[1:]:
-        for axis in (0, 1):
+    for axis in (0, 1):
+        for a in (1, 3):
             rows_copy(axis, a).wait_send()
+            rows_onward(axis, a == 1).wait_send()
+        for a in RING[1:]:
             tabs_copy(axis, a).wait_send()
     for copy in w_copies:
         copy.wait()

time: 381 us -> 356 us (0.934); the launches traced: 373 us -> 356 us
  Pallas kernels: 370 us -> 353 us
    pallas_call x1, Pallas kernels: 370 us -> 353 us  [local_layer(): pl.pallas_call(functools.partial(moe_kernel, n, cap_p), out_shape=jax.Sha...]
where the time goes in v4:
time: 356 us
  Pallas kernels  353 us (99%)
    pallas_call x1, Pallas kernels, local_layer(): pl.pallas_call(functools.partial(moe_kernel, n, cap_p), out_shape=jax.Sha...  353 us

profile of v4, /device:TPU:106, one launch (start us, length us, event | category | flops | bytes accessed | tf_op | source)
XLA Modules:
  0.0 356.0 jit_solution(7080631272842515420)
XLA Ops:
  0.0 352.9 %shard_map.82 = bf16[1024,1024]{1,0:T(8,128)(2,1)} custom-call(bf16[1024,1024]{1,0:T(8,128)(2,1)} %x_ref.1, s32[8,1024]{1,0:T(8,128)} %bitcast.4, f32[8,1024]{1,0:T(8,128)} %bitcast.5, s32[1,1024]{1,0:T(1,128)} %bitcast.6, f32[1,1024]{1,0:T(1,128)} %bitcast.7, bf16[1,1024,512]{2,1,0:T(8,128)(2,1)} %wg_ref.1, bf16[1,1024,512]{2,1,0:T(8,128)(2,1)} %wu_ref.1, ...), custom_call_target="tpu_custom_call" | custom-call | tf_op jit(solution)/shard_map/pallas_call | solution.py:475
  352.9 3.1 copy.10

commit v5 on v4

--- a/solution.py
+++ b/solution.py
@@ -37,8 +37,8 @@
     return dx, dy, lax.rem(t, 2)
 
 
-def moe_kernel(n, cap_p, x_ref, ids_ref, gates_ref, hot_tok_ref, hot_g_ref, wg_ref, wu_ref, wd_ref, out_ref,
-               own, hot, xbuf, hbuf, ring_x, ring_y, tab_x, tab_y, slot_t, gate_t, slot_r, slot_x, hot_w, acc,
+def moe_kernel(n, cap_p, x_hbm, ids_ref, gates_ref, hot_tok_ref, hot_g_ref, wg_ref, wu_ref, wd_ref, out_ref,
+               x_ref, own, hot, xbuf, hbuf, ring_x, ring_y, tab_x, tab_y, slot_t, gate_t, slot_r, slot_x, hot_w, acc,
                w_sem, s1_send, s1_recv, s2_send, s2_recv, s3_send, s3_recv,
                rows_send, rows_recv, tabs_send, tabs_recv, part_send, part_recv, h1_send, h1_recv, h2_send, h2_recv, out_sem, free, ready):
     tokens, d_model = x_ref.shape
@@ -66,6 +66,8 @@
         return pltpu.make_async_remote_copy(src_ref=src, dst_ref=dst, send_sem=send, recv_sem=recv,
                                             device_id={'ep': device}, device_id_type=MESH)
 
+    x_in = pltpu.make_async_copy(x_hbm, x_ref, w_sem.at[3])
+    x_in.start()
     barrier = pltpu.get_barrier_semaphore()
 
     def greet(k, c):
@@ -78,9 +80,8 @@
         pltpu.make_async_copy(wu_ref.at[0], own.at[pl.ds(0, d_model), pl.ds(d_ff, d_ff)], w_sem.at[1]),
         pltpu.make_async_copy(wd_ref.at[0], own.at[pl.ds(d_model, d_ff), :], w_sem.at[2]),
     )
-    for copy in w_copies:
-        copy.start()
     pl.semaphore_wait(barrier, n - 1)
+    x_in.wait()
 
     cols = (pl.ds(0, wide), pl.ds(wide, wide))
     rings = (ring_x, ring_y)
@@ -110,6 +111,9 @@
     for a in (1, 3):
         for axis in (0, 1):
             rows_copy(axis, a).start()
+
+    for copy in w_copies:
+        copy.start()
 
     expert = lax.broadcasted_iota(jnp.int32, (lanes, tokens), 0)
     chosen = jnp.zeros((lanes, tokens), F32)
@@ -363,14 +367,16 @@
     own_lane = lax.broadcasted_iota(jnp.int32, (tile, lanes), 1)
     pos_lane = lax.broadcasted_iota(jnp.int32, (tile, cap_p), 1).astype(F32)
 
+    def weighted(e, rows, at):
+        mine = own_lane == e
+        place = jnp.sum(jnp.where(mine, slot_t[at, :], 0.0), axis=1, keepdims=True)
+        gate = jnp.sum(jnp.where(mine, gate_t[at, :], 0.0), axis=1, keepdims=True)
+        pick = jnp.where(pos_lane == place, 1.0, 0.0).astype(BF16)
+        acc[at, :] += gate * jnp.dot(pick, rows[...], preferred_element_type=F32)
+
     def combine(e, rows):
         def body(i, c):
-            at = pl.ds(pl.multiple_of(i * tile, tile), tile)
-            mine = own_lane == e
-            place = jnp.sum(jnp.where(mine, slot_t[at, :], 0.0), axis=1, keepdims=True)
-            gate = jnp.sum(jnp.where(mine, gate_t[at, :], 0.0), axis=1, keepdims=True)
-            pick = jnp.where(pos_lane == place, 1.0, 0.0).astype(BF16)
-            acc[at, :] += gate * jnp.dot(pick, rows[...], preferred_element_type=F32)
+            weighted(e, rows, pl.ds(pl.multiple_of(i * tile, tile), tile))
             return c
         lax.fori_loop(0, tiles, body, 0)
 
@@ -428,9 +434,13 @@
                 @pl.when(steps == 0)
                 def _():
                     hbuf[q, :, cols[axis]] = xbuf[q, :, cols[axis]]
-            combine(maker, hbuf.at[q])
+
+            @pl.when(t < n - 1)
+            def _():
+                combine(maker, hbuf.at[q])
         return c
     lax.fori_loop(1, n, combine_step, 0)
+    final = place_of(ARRIVALS, jnp.int32(n - 1))
 
     @pl.when(me == 0)
     def _():
@@ -444,6 +454,9 @@
         return pltpu.make_async_copy(rings[axis].at[0, at, :], out_ref.at[at, cols[axis]], out_sem.at[axis, i])
 
     for i in range(tiles):
+        @pl.when(dev(*final) != 0)
+        def _():
+            weighted(dev(*final), hbuf.at[slot_of(*final)], pl.ds(i * tile, tile))
         for axis in (0, 1):
             rings[axis][0, pl.ds(i * tile, tile), :] = acc[pl.ds(i * tile, tile), cols[axis]].astype(BF16)
             if i:
@@ -475,9 +488,10 @@
         return pl.pallas_call(
             functools.partial(moe_kernel, n, cap_p),
             out_shape=jax.ShapeDtypeStruct((tokens, d_model), BF16),
-            in_specs=[vmem] * 5 + [hbm] * 3,
+            in_specs=[hbm] + [vmem] * 4 + [hbm] * 3,
             out_specs=hbm,
             scratch_shapes=[
+                pltpu.VMEM((tokens, d_model), BF16),
                 pltpu.VMEM((d_model + d_ff, d_model), BF16),
                 pltpu.VMEM((d_model + d_ff, d_model), BF16),
                 pltpu.VMEM((n, cap_p, d_model), BF16),
@@ -492,7 +506,7 @@
                 pltpu.VMEM((n, tokens), F32),
                 pltpu.VMEM((tokens, 1), F32),
                 pltpu.VMEM((tokens, d_model), F32),
-                dma((3,)), dma((n,)), dma, dma((2, half - 1)), dma((2, half - 1)), dma, dma,
+                dma((4,)), dma((n,)), dma, dma((2, half - 1)), dma((2, half - 1)), dma, dma,
                 dma((2, SIDE)), dma((2, SIDE)), dma((2, SIDE)), dma((2, SIDE)),
                 dma((2, n)), dma((2, n)), dma((2, n)), dma((2, n)), dma((2, n)), dma((2, n)), dma((2, tokens // 256)),
                 pltpu.SemaphoreType.REGULAR((2, n)), pltpu.SemaphoreType.REGULAR((2, n)),

time: 356 us -> 355 us (level)
  no operation moved by 1% of the time
where the time goes in v5:
time: 355 us
  Pallas kernels  352 us (99%)
    pallas_call x1, Pallas kernels, local_layer(): pl.pallas_call(functools.partial(moe_kernel, n, cap_p), out_shape=jax.Sha...  352 us

profile of v5, /device:TPU:106, one launch (start us, length us, event | category | flops | bytes accessed | tf_op | source)
XLA Modules:
  0.0 355.0 jit_solution(7645124660662967217)
XLA Ops:
  0.0 351.9 %shard_map.82 = bf16[1024,1024]{1,0:T(8,128)(2,1)} custom-call(bf16[1024,1024]{1,0:T(8,128)(2,1)} %x_hbm.1, s32[8,1024]{1,0:T(8,128)} %bitcast.4, f32[8,1024]{1,0:T(8,128)} %bitcast.5, s32[1,1024]{1,0:T(1,128)} %bitcast.6, f32[1,1024]{1,0:T(1,128)} %bitcast.7, bf16[1,1024,512]{2,1,0:T(8,128)(2,1)} %wg_ref.1, bf16[1,1024,512]{2,1,0:T(8,128)(2,1)} %wu_ref.1, ...), custom_call_target="tpu_custom_call" | custom-call | tf_op jit(solution)/shard_map/pallas_call | solution.py:488
  351.9 3.1 copy.10
